TPU v7x, 256 devices: a whole 4x4x8 slice. The times are simulated.
256 devices in a mesh: row: 32 (over x, y, core), col: 8 (over z).
Axes of the slice: x: 4, y: 4, z: 8, core: 2. Of those that a mesh axis runs over, the one named last changes fastest.
Arguments:
- matrix: float32 [5120, 5120], P('row', 'col'), may hold values from -64 to 64
Outputs:
- iterate: float32 [5120, 5120], P('row', 'col')
- trace_value: float32 [2], replicated
- frobenius: float32 [2], replicated
All inputs are finite; a program needn't handle non-finite values.
Results may differ from a plain program's by a relative error of at most 0.003.
Values may be sent and summed in bfloat16 or wider, within the bound.
No kernel may reach another device: no remote copies, remote signals or barrier semaphores. Data moves between devices by JAX's collectives and lax.ppermute only.
A program may use at most 64 MiB of HBM per device.

v0:
```python
import jax
import jax.numpy as jnp
from jax import lax
from jax.sharding import Mesh
from jax.sharding import PartitionSpec as P

ITERS = 2
ROW = ("row_0", "row_1", "row_2")
ROW_COL = ("row_0", "row_1", "row_2", "col")
target = 0.0625


def from_everyone(shard, axis):
    peers = lax.axis_size(axis)
    return lax.all_to_all(
        jnp.broadcast_to(shard[None], (peers, *shard.shape)), axis, 0, 0, tiled=True
    )


def in_order(pieces, dim):
    shape = list(pieces.shape[1:])
    shape[dim] *= pieces.shape[0]
    return jnp.moveaxis(pieces, 0, dim).reshape(shape)


def collect(shard, axis, dim):
    pieces = from_everyone(shard, axis)
    return in_order(pieces, dim)


def over_axes(shard, axes):
    for axis in axes:
        shard = lax.psum(shard, axis)
    return shard


def add_rows(portion, right_panel):
    return jnp.dot(portion, right_panel, preferred_element_type=jnp.float32)


def on_device(matrix):
    rounded = matrix.astype(jnp.bfloat16)
    current = rounded.astype(jnp.float32)
    row_ids = lax.axis_index(ROW) * matrix.shape[0] + lax.broadcasted_iota(
        jnp.int32, matrix.shape, 0
    )
    col_ids = lax.axis_index("col") * matrix.shape[1] + lax.broadcasted_iota(
        jnp.int32, matrix.shape, 1
    )
    on_diagonal = row_ids == col_ids
    traces = []
    norms = []
    for step in range(ITERS):
        row_panel = collect(rounded, "col", 1)
        if step == 0:
            order_full = row_panel.shape[1]
            squares = over_axes(jnp.sum(current * current), ROW_COL)
            scale = target * order_full / (squares + 1e-06)
            root = jnp.sqrt(scale)
        else:
            scale = jnp.float32(1.0)
            root = jnp.float32(1.0)
        kept_panel = lax.all_gather(rounded, ROW, axis=0, tiled=True)
        product = jnp.dot(row_panel, kept_panel, preferred_element_type=jnp.float32)
        squared = (product * scale).astype(jnp.bfloat16)
        cubic_part = add_rows(
            lax.all_gather(squared, "col", axis=1, tiled=True), right_panel=kept_panel
        )
        current = root * (1.5 * current - 0.5 * cubic_part)
        rounded = current.astype(jnp.bfloat16)
        diagonal_part = jnp.sum(jnp.where(on_diagonal, current, 0.0))
        square_part = jnp.sum(current * current)
        trace_now, total_now = (over_axes(diagonal_part, ROW_COL), over_axes(square_part, ROW_COL))
        traces.append(trace_now)
        norms.append(jnp.sqrt(total_now))
    return (current, jnp.stack(traces), jnp.stack(norms))


def solution(mesh):
    split = Mesh(
        mesh.devices.reshape(4, 4, 2, mesh.shape["col"]), ("row_0", "row_1", "row_2", "col")
    )
    return jax.shard_map(
        on_device,
        mesh=split,
        in_specs=(P(ROW, "col"),),
        out_specs=(P(ROW, "col"), P(), P()),
        check_vma=False,
    )
```

profile of v0, /device:TPU:32, one launch (start us, length us, event | category | flops | bytes accessed | tf_op | source)
XLA Modules:
  0.0 274.8 jit_solution(13605825605742799116)
XLA Ops:
  7.2 0.0 all-gather.5.cloned.1.call-start
  7.2 2.3 fusion.4
  9.5 0.0 all-gather.5.cloned.1.call-update
  9.5 2.2 broadcast_in_dim.9
  11.8 8.6 %all-to-all-start = ((bf16[8,160,640]{2,1,0:T(8,128)(2,1)}), bf16[8,160,640]{2,1,0:T(8,128)(2,1)S(1)}, u32[]{:S(2)}, u32[]{:S(2)}) async-start(bf16[8,160,640]{2,1,0:T(8,128)(2,1)} %broadcast_in_dim.9), calls=%async_computation | async-start | bytes 3276800 | tf_op jit(solution)/shard_map/all_to_all | solution.py:15
  20.4 11.1 %psum.140 = f32[]{:T(128)} all-reduce(f32[]{:T(128)} %get-tuple-element.23), channel_id=1, replica_groups=mesh['row_0'=4,'row_1'=4,'row_2'=2,'col'=8] {'row_0'}, use_global_device_ids=true, to_apply=%region_1.0 | all-reduce | flops 1 | bytes 8 | tf_op jit(solution)/shard_map/psum | solution.py:33
  31.5 11.4 %psum.141 = f32[]{:T(128)} all-reduce(f32[]{:T(128)} %psum.140), channel_id=1, replica_groups=mesh['row_0'=4,'row_1'=4,'row_2'=2,'col'=8] {'row_1'}, use_global_device_ids=true, to_apply=%region_2.0 | all-reduce | flops 1 | bytes 8 | tf_op jit(solution)/shard_map/psum | solution.py:33
  42.8 3.1 %psum.142 = f32[]{:T(128)} all-reduce(f32[]{:T(128)} %psum.141), channel_id=1, replica_groups=mesh['row_0'=4,'row_1'=4,'row_2'=2,'col'=8] {'row_2'}, use_global_device_ids=true, to_apply=%region_3.0 | all-reduce | flops 1 | bytes 8 | tf_op jit(solution)/shard_map/psum | solution.py:33
  45.9 20.6 %psum.143 = f32[]{:T(128)} all-reduce(f32[]{:T(128)} %psum.142), channel_id=1, replica_groups=mesh['row_0'=4,'row_1'=4,'row_2'=2,'col'=8] {'col'}, use_global_device_ids=true, to_apply=%region_4.0 | all-reduce | flops 1 | bytes 8 | tf_op jit(solution)/shard_map/psum | solution.py:33
  67.2 0.0 all-to-all-done
  67.2 0.2 copy.6
  67.5 0.7 all-gather.5.cloned.1.call-done
  68.2 5.0 %fusion.3 = bf16[160,640]{1,0:T(8,128)(2,1)} fusion(bf16[160,5120]{1,0:T(8,128)(2,1)S(1)} %bitcast.18, bf16[5120,640]{1,0:T(8,128)(2,1)} %all-gather.5.cloned.1.call-done, f32[]{:T(128)S(6)} %div.3), kind=kOutput, calls=%fused_computation.6 | convolution fusion | flops 1048780800 | bytes 8396804 | tf_op jit(solution)/shard_map/dot_general | solution.py:64
  73.2 0.0 all-gather.7.cloned.1.call-update
  73.2 0.0 all-gather.9.cloned.1.call-start
  73.3 41.0 %all-gather.7.cloned.1.call-done = bf16[160,5120]{1,0:T(8,128)(2,1)} async-done(((bf16[160,640]{1,0:T(8,128)(2,1)}), bf16[160,5120]{1,0:T(8,128)(2,1)}) %all-gather.7.cloned.1.call-update) | async-done | bytes 1638416 | tf_op jit(solution)/shard_map/all_gather | solution.py:67
  114.3 6.1 %multiply_reduce_fusion.1 = (f32[]{:T(128)}, f32[]{:T(128)}, bf16[160,640]{1,0:T(8,128)(2,1)}, f32[160,640]{1,0:T(8,128)S(1)}) fusion(s32[640]{0:T(1024)S(1)} %iota_add_fusion, s32[160]{0:T(256)S(1)} %iota_add_fusion.1, bf16[160,5120]{1,0:T(8,128)(2,1)} %all-gather.7.cloned.1.call-done, bf16[5120,640]{1,0:T(8,128)(2,1)} %all-gather.5.cloned.1.call-done, ...), kind=kOutput, calls=%fused_computation.16 | convolution fusion | flops 1049702400 | bytes 9014412 | tf_op jit(solution)/shard_map/dot_general | solution.py:38
  120.5 0.0 all-gather.9.cloned.1.call-update
  120.5 0.0 all-gather.11.cloned.1.call-start
  120.5 1.1 broadcast_in_dim.18
  121.6 40.6 %all_to_all.10 = bf16[8,160,640]{2,1,0:T(8,128)(2,1)S(1)} all-to-all(bf16[8,160,640]{2,1,0:T(8,128)(2,1)S(1)} %broadcast_in_dim.18), channel_id=1, replica_groups=mesh['row_0'=4,'row_1'=4,'row_2'=2,'col'=8] {'col'}, dimensions={0} | all-to-all | bytes 3276800 | tf_op jit(solution)/shard_map/all_to_all | solution.py:15
  162.2 0.2 copy.7
  162.4 11.6 %all-gather.9.cloned.1.call-done = bf16[5120,640]{1,0:T(8,128)(2,1)} async-done(((bf16[160,640]{1,0:T(8,128)(2,1)}), bf16[5120,640]{1,0:T(8,128)(2,1)}) %all-gather.9.cloned.1.call-update) | async-done | bytes 6553616 | tf_op jit(solution)/shard_map/all_gather | solution.py:63
  174.0 5.0 %convolution_convert_fusion = bf16[160,640]{1,0:T(8,128)(2,1)} fusion(bf16[160,5120]{1,0:T(8,128)(2,1)S(1)} %bitcast.19, bf16[5120,640]{1,0:T(8,128)(2,1)} %all-gather.9.cloned.1.call-done), kind=kOutput, calls=%fused_computation.7 | convolution fusion | flops 1048678400 | bytes 8396800 | tf_op jit(solution)/shard_map/dot_general | solution.py:64
  179.0 0.0 all-gather.11.cloned.1.call-update
  179.0 38.3 %all-gather.11.cloned.1.call-done = bf16[160,5120]{1,0:T(8,128)(2,1)} async-done(((bf16[160,640]{1,0:T(8,128)(2,1)}), bf16[160,5120]{1,0:T(8,128)(2,1)}) %all-gather.11.cloned.1.call-update) | async-done | bytes 1638416 | tf_op jit(solution)/shard_map/all_gather | solution.py:67
  217.3 6.2 %multiply_reduce_fusion = (f32[]{:T(128)}, f32[]{:T(128)}, f32[160,640]{1,0:T(8,128)}) fusion(s32[640]{0:T(1024)S(1)} %iota_add_fusion, s32[160]{0:T(256)S(1)} %iota_add_fusion.1, bf16[160,5120]{1,0:T(8,128)(2,1)} %all-gather.11.cloned.1.call-done, bf16[5120,640]{1,0:T(8,128)(2,1)} %all-gather.9.cloned.1.call-done, f32[160,640]{1,0:T(8,128)S(1)} %get-tuple-element.26), kind=kOutput, calls=%fused_computation.15 | convolution fusion | flops 1049395200 | bytes 9014408 | tf_op jit(solution)/shard_map/dot_general | solution.py:38
  223.5 11.1 %all-reduce.2 = (f32[]{:T(128)}, f32[]{:T(128)}, f32[]{:T(128)}, f32[]{:T(128)}) all-reduce(f32[]{:T(128)} %get-tuple-element.6, f32[]{:T(128)} %get-tuple-element.4, f32[]{:T(128)} %get-tuple-element.5, f32[]{:T(128)} %get-tuple-element.3), channel_id=1, replica_groups=mesh['row_0'=4,'row_1'=4,'row_2'=2,'col'=8] {'row_0'}, use_global_device_ids=true, to_apply=%region_11.12 | all-reduce | flops 4 | bytes 32 | tf_op jit(solution)/shard_map/psum | solution.py:33
  234.6 11.1 %all-reduce.1 = (f32[]{:T(128)}, f32[]{:T(128)}, f32[]{:T(128)}, f32[]{:T(128)}) all-reduce(f32[]{:T(128)} %get-tuple-element.15, f32[]{:T(128)} %get-tuple-element.16, f32[]{:T(128)} %get-tuple-element.17, f32[]{:T(128)} %get-tuple-element.18), channel_id=1, replica_groups=mesh['row_0'=4,'row_1'=4,'row_2'=2,'col'=8] {'row_1'}, use_global_device_ids=true, to_apply=%region_12.13 | all-reduce | flops 4 | bytes 32 | tf_op jit(solution)/shard_map/psum | solution.py:33
  245.7 3.2 %all-reduce.3 = (f32[]{:T(128)}, f32[]{:T(128)}, f32[]{:T(128)}, f32[]{:T(128)}) all-reduce(f32[]{:T(128)} %get-tuple-element.11, f32[]{:T(128)} %get-tuple-element.12, f32[]{:T(128)} %get-tuple-element.13, f32[]{:T(128)} %get-tuple-element.14), channel_id=1, replica_groups=mesh['row_0'=4,'row_1'=4,'row_2'=2,'col'=8] {'row_2'}, use_global_device_ids=true, to_apply=%region_13.14 | all-reduce | flops 4 | bytes 32 | tf_op jit(solution)/shard_map/psum | solution.py:33
  248.9 16.1 %all-reduce = (f32[1]{0:T(128)}, f32[1]{0:T(128)}, f32[]{:T(128)}, f32[]{:T(128)}) all-reduce(f32[1]{0:T(128)} %bitcast.3, f32[1]{0:T(128)} %bitcast.2, f32[]{:T(128)} %get-tuple-element.21, f32[]{:T(128)} %get-tuple-element.22), channel_id=1, replica_groups=mesh['row_0'=4,'row_1'=4,'row_2'=2,'col'=8] {'col'}, use_global_device_ids=true, to_apply=%region_14.15 | all-reduce | flops 4 | bytes 32 | tf_op jit(solution)/shard_map/psum | solution.py:33
  266.4 1.9 pad_maximum_fusion
  (5 shorter events, 0.0 us)
Async XLA Ops:
  7.2 61.0 %all-gather.5.cloned.1.call-start = ((), (), s32[]{:S(2)}) async-start(), calls=%async_computation.2 | async-start | bytes 6758400 | tf_op jit(solution)/shard_map/all_gather | solution.py:63
  11.8 55.4 %all-to-all-start = ((bf16[8,160,640]{2,1,0:T(8,128)(2,1)}), bf16[8,160,640]{2,1,0:T(8,128)(2,1)S(1)}, u32[]{:S(2)}, u32[]{:S(2)}) async-start(bf16[8,160,640]{2,1,0:T(8,128)(2,1)} %broadcast_in_dim.9), calls=%async_computation | async-start | bytes 3276800 | tf_op jit(solution)/shard_map/all_to_all | solution.py:15
  20.3 94.0 %all-gather.7.cloned.1.call-start = ((), (), s32[]{:S(2)}) async-start(), calls=%async_computation.3 | async-start | bytes 1843200 | tf_op jit(solution)/shard_map/all_gather | solution.py:67
  68.2 46.2 %copy-start = (bf16[160,640]{1,0:T(8,128)(2,1)S(1)}, bf16[160,640]{1,0:T(8,128)(2,1)}, u32[]{:S(2)}) copy-start(bf16[160,640]{1,0:T(8,128)(2,1)} %get-tuple-element.24) | copy-start | bytes 614404
  73.2 100.8 %all-gather.9.cloned.1.call-start = ((), (), s32[]{:S(2)}) async-start(), calls=%async_computation.4 | async-start | bytes 6758400 | tf_op jit(solution)/shard_map/all_gather | solution.py:63
  120.5 96.8 %all-gather.11.cloned.1.call-start = ((), (), s32[]{:S(2)}) async-start(), calls=%async_computation.5 | async-start | bytes 1843200 | tf_op jit(solution)/shard_map/all_gather | solution.py:67
Sparse Core Ops, SparseCore 0:
  11.1 57.0 all-gather.4
  73.3 40.9 all-gather.6
  120.6 53.3 all-gather.8
  179.2 38.0 all-gather.10
where the time goes:
time: 275 us
  blocking collectives  128 us (47%)
  waiting for transfers between devices  91.6 us (33%)
  matrix products  22.3 us (8%)
  between operations  15.9 us (6%)
  starting transfers between devices  8.69 us (3%)
  other arithmetic  4.18 us (2%)
  local copies, waits for them, and re-layouts  3.75 us (1%)
    psum x8, blocking collectives, over_axes(): shard = lax.psum(shard, axis)  87.7 us
    all_gather x2, waiting for transfers between devices, on_device(): lax.all_gather(squared, 'col', axis=1, tiled=True)  79.2 us
    all_to_all x1, blocking collectives, from_everyone(): lax.all_to_all(jnp.broadcast_to(shard[None], (peers, *shard.shape)), axis...  40.6 us
    dot_general x2, matrix products, add_rows(): return jnp.dot(portion, right_panel, preferred_element_type=jnp.float32)  12.3 us
    all_gather x2, waiting for transfers between devices, on_device(): kept_panel = lax.all_gather(rounded, ROW, axis=0, tiled=True)  12.3 us
    dot_general x2, matrix products, on_device(): product = jnp.dot(row_panel, kept_panel, preferred_element_type=jnp.float32)  10 us
    all_to_all x1, starting transfers between devices, from_everyone(): lax.all_to_all(jnp.broadcast_to(shard[None], (peers, *shard.shape)), axis...  8.57 us
  transfers between devices with their start and end apart: 5, of which 4 were waited for; matrix products, arithmetic and copies ran while one was open for 1% of the time, Pallas kernels for 0%

commit v1 on v0

--- a/solution.py
+++ b/solution.py
@@ -30,7 +30,8 @@
 
 def over_axes(shard, axes):
     for axis in axes:
-        shard = lax.psum(shard, axis)
+        shards = lax.all_gather(shard, axis)
+        shard = jnp.sum(shards, axis=0)
     return shard
 
 

time: 275 us -> 302 us (1.098)
  local copies, waits for them, and re-layouts: 3.75 us -> 33.5 us
  other arithmetic: 4.18 us -> 16.2 us
  blocking collectives: 128 us -> 119 us
  waiting for transfers between devices: 91.6 us -> 85.6 us
    psum x8 -> x0, blocking collectives: 87.7 us -> none  [over_axes(): shard = lax.psum(shard, axis)]
    unnamed x0 -> x8, blocking collectives: none -> 77.9 us
    unnamed x2 -> x54, local copies, waits for them, and re-layouts: 0.01 us -> 29.8 us
    reduce_sum x0 -> x20, other arithmetic: none -> 12.1 us  [over_axes(): shard = jnp.sum(shards, axis=0)]
    all_gather x2, waiting for transfers between devices: 79.2 us -> 73.9 us  [on_device(): lax.all_gather(squared, 'col', axis=1, tiled=True)]
  transfers between devices with their start and end apart: 5 -> 5, of which waited for: 4 -> 3; matrix products, arithmetic and copies ran while one was open for 1% -> 6% of each run, Pallas kernels for 0% -> 0%
where the time goes in v1:
time: 302 us; the launch traced here: 301 us
  blocking collectives  119 us (39%)
  waiting for transfers between devices  85.6 us (28%)
  local copies, waits for them, and re-layouts  33.5 us (11%)
  matrix products  22.4 us (7%)
  other arithmetic  16.2 us (5%)
  between operations  16 us (5%)
  starting transfers between devices  8.84 us (3%)
    unnamed x8, blocking collectives  77.9 us
    all_gather x2, waiting for transfers between devices, on_device(): lax.all_gather(squared, 'col', axis=1, tiled=True)  73.9 us
    all_to_all x1, blocking collectives, from_everyone(): lax.all_to_all(jnp.broadcast_to(shard[None], (peers, *shard.shape)), axis...  40.6 us
    unnamed x54, local copies, waits for them, and re-layouts  29.8 us
    dot_general x2, matrix products, add_rows(): return jnp.dot(portion, right_panel, preferred_element_type=jnp.float32)  12.3 us
    reduce_sum x20, other arithmetic, over_axes(): shard = jnp.sum(shards, axis=0)  12.1 us
    all_gather x2, waiting for transfers between devices, on_device(): kept_panel = lax.all_gather(rounded, ROW, axis=0, tiled=True)  11.6 us
    dot_general x2, matrix products, on_device(): product = jnp.dot(row_panel, kept_panel, preferred_element_type=jnp.float32)  10.1 us
  transfers between devices with their start and end apart: 5, of which 3 were waited for; matrix products, arithmetic and copies ran while one was open for 6% of the time, Pallas kernels for 0%

profile of v1, /device:TPU:32, one launch (start us, length us, event | category | flops | bytes accessed | tf_op | source)
XLA Modules:
  0.0 301.1 jit_solution(14554605420120814608)
XLA Ops:
  7.2 2.3 fusion.4
  9.5 2.2 broadcast_in_dim.9
  11.8 8.7 %all-to-all-start = ((bf16[8,160,640]{2,1,0:T(8,128)(2,1)}), bf16[8,160,640]{2,1,0:T(8,128)(2,1)S(1)}, u32[]{:S(2)}, u32[]{:S(2)}) async-start(bf16[8,160,640]{2,1,0:T(8,128)(2,1)} %broadcast_in_dim.9), calls=%async_computation | async-start | bytes 3276800 | tf_op jit(solution)/shard_map/all_to_all | solution.py:15
  21.1 1.4 dynamic-update-slice
  22.5 10.5 %all-reduce = f32[4]{0:T(128)S(1)} all-reduce(f32[4]{0:T(128)S(1)} %dynamic-update-slice), channel_id=1, replica_groups=mesh['row_0'=4,'row_1'=4,'row_2'=2,'col'=8] {'row_0'}, use_global_device_ids=true, to_apply=%add | all-reduce | flops 4 | bytes 32
  34.2 1.4 dynamic-update-slice.1
  35.5 10.7 %all-reduce.1 = f32[4]{0:T(128)S(1)} all-reduce(f32[4]{0:T(128)S(1)} %dynamic-update-slice.1), channel_id=1, replica_groups=mesh['row_0'=4,'row_1'=4,'row_2'=2,'col'=8] {'row_1'}, use_global_device_ids=true, to_apply=%add.1 | all-reduce | flops 4 | bytes 32
  48.8 2.4 all-reduce.2
  52.4 1.4 dynamic-update-slice.3
  53.8 15.6 %all-reduce.3 = f32[8]{0:T(128)S(1)} all-reduce(f32[8]{0:T(128)S(1)} %dynamic-update-slice.3), channel_id=1, replica_groups=mesh['row_0'=4,'row_1'=4,'row_2'=2,'col'=8] {'col'}, use_global_device_ids=true, to_apply=%add.3 | all-reduce | flops 8 | bytes 64
  71.0 5.0 %fusion.3 = bf16[160,640]{1,0:T(8,128)(2,1)} fusion(bf16[160,5120]{1,0:T(8,128)(2,1)S(1)} %bitcast.42, bf16[5120,640]{1,0:T(8,128)(2,1)} %all-gather.5.cloned.1.call-done, f32[]{:T(128)S(6)} %div.3), kind=kOutput, calls=%fused_computation.6 | convolution fusion | flops 1048780800 | bytes 8396804 | tf_op jit(solution)/shard_map/dot_general | solution.py:65
  76.2 38.4 %all-gather.7.cloned.1.call-done = bf16[160,5120]{1,0:T(8,128)(2,1)} async-done(((bf16[160,640]{1,0:T(8,128)(2,1)}), bf16[160,5120]{1,0:T(8,128)(2,1)}) %all-gather.7.cloned.1.call-update) | async-done | bytes 1638416 | tf_op jit(solution)/shard_map/all_gather | solution.py:68
  114.6 6.1 %multiply_reduce_fusion.1 = (f32[]{:T(128)}, f32[]{:T(128)}, bf16[160,640]{1,0:T(8,128)(2,1)}, f32[160,640]{1,0:T(8,128)S(1)}) fusion(s32[640]{0:T(1024)S(1)} %iota_add_fusion, s32[160]{0:T(256)S(1)} %iota_add_fusion.1, bf16[160,5120]{1,0:T(8,128)(2,1)} %all-gather.7.cloned.1.call-done, bf16[5120,640]{1,0:T(8,128)(2,1)} %all-gather.5.cloned.1.call-done, ...), kind=kOutput, calls=%fused_computation.16 | convolution fusion | flops 1049702400 | bytes 9014412 | tf_op jit(solution)/shard_map/dot_general | solution.py:39
  121.9 40.6 %all_to_all.10 = bf16[8,160,640]{2,1,0:T(8,128)(2,1)S(1)} all-to-all(bf16[8,160,640]{2,1,0:T(8,128)(2,1)S(1)} %broadcast_in_dim.18), channel_id=1, replica_groups=mesh['row_0'=4,'row_1'=4,'row_2'=2,'col'=8] {'col'}, dimensions={0} | all-to-all | bytes 3276800 | tf_op jit(solution)/shard_map/all_to_all | solution.py:15
  162.7 11.6 %all-gather.9.cloned.1.call-done = bf16[5120,640]{1,0:T(8,128)(2,1)} async-done(((bf16[160,640]{1,0:T(8,128)(2,1)}), bf16[5120,640]{1,0:T(8,128)(2,1)}) %all-gather.9.cloned.1.call-update) | async-done | bytes 6553616 | tf_op jit(solution)/shard_map/all_gather | solution.py:64
  174.3 5.0 %convolution_convert_fusion = bf16[160,640]{1,0:T(8,128)(2,1)} fusion(bf16[160,5120]{1,0:T(8,128)(2,1)S(1)} %bitcast.43, bf16[5120,640]{1,0:T(8,128)(2,1)} %all-gather.9.cloned.1.call-done), kind=kOutput, calls=%fused_computation.7 | convolution fusion | flops 1048678400 | bytes 8396800 | tf_op jit(solution)/shard_map/dot_general | solution.py:65
  179.4 1.4 dynamic-update-slice.4
  180.7 1.4 dynamic-update-slice.12
  182.2 35.5 %all-gather.11.cloned.1.call-done = bf16[160,5120]{1,0:T(8,128)(2,1)} async-done(((bf16[160,640]{1,0:T(8,128)(2,1)}), bf16[160,5120]{1,0:T(8,128)(2,1)}) %all-gather.11.cloned.1.call-update) | async-done | bytes 1638416 | tf_op jit(solution)/shard_map/all_gather | solution.py:68
  217.6 6.2 %multiply_reduce_fusion = (f32[]{:T(128)}, f32[]{:T(128)}, f32[160,640]{1,0:T(8,128)}) fusion(s32[640]{0:T(1024)S(1)} %iota_add_fusion, s32[160]{0:T(256)S(1)} %iota_add_fusion.1, bf16[160,5120]{1,0:T(8,128)(2,1)} %all-gather.11.cloned.1.call-done, bf16[5120,640]{1,0:T(8,128)(2,1)} %all-gather.9.cloned.1.call-done, f32[160,640]{1,0:T(8,128)S(1)} %get-tuple-element.26), kind=kOutput, calls=%fused_computation.15 | convolution fusion | flops 1049395200 | bytes 9014408 | tf_op jit(solution)/shard_map/dot_general | solution.py:39
  223.8 1.4 dynamic-update-slice.8
  225.2 1.4 dynamic-update-slice.16
  226.6 10.4 %all-reduce.22 = (f32[4]{0:T(128)S(1)}, f32[4]{0:T(128)S(1)}, f32[4]{0:T(128)S(1)}, f32[4]{0:T(128)S(1)}) all-reduce(f32[4]{0:T(128)S(1)} %dynamic-update-slice.8, f32[4]{0:T(128)S(1)} %dynamic-update-slice.4, f32[4]{0:T(128)S(1)} %dynamic-update-slice.16, ...), channel_id=1, replica_groups=mesh['row_0'=4,'row_1'=4,'row_2'=2,'col'=8] {'row_0'}, use_global_device_ids=true, to_apply=%add.8 | all-reduce | flops 16 | bytes 128
  237.6 1.4 dynamic-update-slice.9
  239.6 1.4 dynamic-update-slice.5
  241.6 1.4 dynamic-update-slice.17
  243.5 1.4 dynamic-update-slice.13
  244.9 10.4 %all-reduce.21 = (f32[4]{0:T(128)S(1)}, f32[4]{0:T(128)S(1)}, f32[4]{0:T(128)S(1)}, f32[4]{0:T(128)S(1)}) all-reduce(f32[4]{0:T(128)S(1)} %dynamic-update-slice.9, f32[4]{0:T(128)S(1)} %dynamic-update-slice.5, f32[4]{0:T(128)S(1)} %dynamic-update-slice.17, ...), channel_id=1, replica_groups=mesh['row_0'=4,'row_1'=4,'row_2'=2,'col'=8] {'row_1'}, use_global_device_ids=true, to_apply=%add.9 | all-reduce | flops 16 | bytes 128
  263.1 2.4 all-reduce.23
  266.1 1.4 dynamic-update-slice.11
  273.4 15.4 %all-reduce.20 = (f32[8]{0:T(128)S(1)}, f32[8]{0:T(128)S(1)}, f32[8]{0:T(128)S(1)}, f32[8]{0:T(128)S(1)}) all-reduce(f32[8]{0:T(128)S(1)} %dynamic-update-slice.11, f32[8]{0:T(128)S(1)} %dynamic-update-slice.7, f32[8]{0:T(128)S(1)} %dynamic-update-slice.19, ...), channel_id=1, replica_groups=mesh['row_0'=4,'row_1'=4,'row_2'=2,'col'=8] {'col'}, use_global_device_ids=true, to_apply=%add.11 | all-reduce | flops 32 | bytes 256
  292.7 1.8 pad_maximum_fusion
  (77 shorter events, 27.0 us)
Async XLA Ops:
  7.2 63.8 %all-gather.5.cloned.1.call-start = ((), (), s32[]{:S(2)}) async-start(), calls=%async_computation.2 | async-start | bytes 6758400 | tf_op jit(solution)/shard_map/all_gather | solution.py:64
  11.8 8.7 %copy-start.4 = (u32[256]{0:T(256)S(1)}, u32[256]{0:T(256)}, u32[]{:S(2)}) copy-start(u32[256]{0:T(256)} %constant.38) | copy-start | bytes 3076
  11.8 21.2 %copy-start.3 = (u32[256]{0:T(256)S(1)}, u32[256]{0:T(256)}, u32[]{:S(2)}) copy-start(u32[256]{0:T(256)} %constant.43) | copy-start | bytes 3076
  11.8 34.5 %copy-start.2 = (u32[256]{0:T(256)S(1)}, u32[256]{0:T(256)}, u32[]{:S(2)}) copy-start(u32[256]{0:T(256)} %constant.48) | copy-start | bytes 3076
  11.8 39.4 %copy-start.1 = (u32[256]{0:T(256)S(1)}, u32[256]{0:T(256)}, u32[]{:S(2)}) copy-start(u32[256]{0:T(256)} %constant.53) | copy-start | bytes 3076
  11.8 58.9 %all-to-all-start = ((bf16[8,160,640]{2,1,0:T(8,128)(2,1)}), bf16[8,160,640]{2,1,0:T(8,128)(2,1)S(1)}, u32[]{:S(2)}, u32[]{:S(2)}) async-start(bf16[8,160,640]{2,1,0:T(8,128)(2,1)} %broadcast_in_dim.9), calls=%async_computation | async-start | bytes 3276800 | tf_op jit(solution)/shard_map/all_to_all | solution.py:15
  20.5 94.1 %all-gather.7.cloned.1.call-start = ((), (), s32[]{:S(2)}) async-start(), calls=%async_computation.3 | async-start | bytes 1843200 | tf_op jit(solution)/shard_map/all_gather | solution.py:68
  71.0 43.6 %copy-start = (bf16[160,640]{1,0:T(8,128)(2,1)S(1)}, bf16[160,640]{1,0:T(8,128)(2,1)}, u32[]{:S(2)}) copy-start(bf16[160,640]{1,0:T(8,128)(2,1)} %get-tuple-element.24) | copy-start | bytes 614404
  76.1 98.2 %all-gather.9.cloned.1.call-start = ((), (), s32[]{:S(2)}) async-start(), calls=%async_computation.4 | async-start | bytes 6758400 | tf_op jit(solution)/shard_map/all_gather | solution.py:64
  120.8 96.9 %all-gather.11.cloned.1.call-start = ((), (), s32[]{:S(2)}) async-start(), calls=%async_computation.5 | async-start | bytes 1843200 | tf_op jit(solution)/shard_map/all_gather | solution.py:68
Sparse Core Ops, SparseCore 0:
  11.1 57.0 all-gather.4
  76.2 38.3 all-gather.6
  120.9 53.3 all-gather.8
  179.5 38.0 all-gather.10
